TPU v7x, 32 devices: a whole 2x2x4 slice. The times are simulated.
32 devices in a mesh: head: 2 (over y), outer: 4 (over z), inner: 4 (over x, core).
Axes of the slice: x: 2, y: 2, z: 4, core: 2. Of those that a mesh axis runs over, the one named last changes fastest.
Arguments:
- queries: bfloat16 [1024, 2048], P('outer', ('head', 'inner')), may hold values from -100 to 100
- keys: bfloat16 [1024, 256], P('outer', 'head'), may hold values from -5 to 5
- values: bfloat16 [1024, 256], P('outer', 'head'), may hold values from -6 to 6
- grad_out: bfloat16 [1024, 2048], P('outer', ('head', 'inner')), may hold values from -24 to 24
- hidden_in: bfloat16 [1024, 8192], P('outer', ('head', 'inner')), may hold values from -6 to 6
- adapter_a: bfloat16 [8192, 16], P(('head', 'inner')), may hold values from -0.0625 to 0.0625
- adapter_b: bfloat16 [16, 256], P(None, 'head'), may hold values from -1.5 to 1.5
- block_order: int32 [8], replicated, may hold values from 0 to 7, each once
- doc_ids: int32 [1024], replicated, may hold values from 0 to 3, never falling along the last dimension, each value on 1 to 512 neighbouring positions
Outputs:
- grad_query: bfloat16 [1024, 2048], P('outer', ('head', 'inner'))
- grad_key: bfloat16 [1024, 256], P('outer', 'head')
- grad_value: bfloat16 [1024, 256], P('outer', 'head')
- grad_a: float32 [8192, 16], P(('head', 'inner'))
- grad_b: float32 [16, 256], P(None, 'head')
Inputs may be any that keep to these rules, and one draw needn't show every extreme that they name: `block_order`: a permutation of the stored blocks. `doc_ids`: never falling along positions; each document has 1 to 512 positions.
All inputs are finite; a program needn't handle non-finite values.
Results may differ from a plain program's by a relative error of at most 0.024.
Values may be sent and summed in bfloat16 or wider, within the bound.
A program may use at most 64 MiB of HBM per device.

v0:
```python
import jax
import jax.numpy as jnp
from jax import lax
from jax.sharding import PartitionSpec as P

HEAD_DIM = 128
NEGATIVE = -1e30


def passed_along(value, axis, steps):
    count = lax.axis_size(axis)
    pairs = [(source, (source + steps) % count) for source in range(count)]
    return lax.ppermute(value, axis, pairs)


def block_meta(block_table, doc_table, block_id, half_rows):
    first_pos = block_table[block_id] * half_rows
    places = first_pos + jnp.arange(half_rows, dtype=jnp.int32)
    owners = lax.dynamic_slice_in_dim(doc_table, first_pos, half_rows, 0)
    return (places, owners)


def joined_meta(first, second):
    return (jnp.concatenate((first[0], second[0]), 0), jnp.concatenate((first[1], second[1]), 0))


def visible(query_meta, key_meta):
    return (key_meta[0][None, :] <= query_meta[0][:, None]) & (
        key_meta[1][None, :] == query_meta[1][:, None]
    )


def tile_scores(query_tile, key_rows, scaling):
    return (
        jnp.einsum("tkgd,skd->kgts", query_tile, key_rows, preferred_element_type=jnp.float32)
        * scaling
    )


def forward_tile(carried, masked, query_tile, key_tile, value_tile, scaling):
    peak_score, totals, summed = carried
    kv_local = query_tile.shape[1]
    key_rows = key_tile.reshape(key_tile.shape[0], kv_local, -1)
    value_rows = value_tile.reshape(value_tile.shape[0], kv_local, -1)
    scores = jnp.where(masked, tile_scores(query_tile, key_rows, scaling), NEGATIVE)
    new_peak = jnp.maximum(peak_score, jnp.max(scores, axis=-1))
    weights = jnp.where(masked, jnp.exp(scores - new_peak[..., None]), 0.0)
    factor = jnp.exp(peak_score - new_peak)
    summed = summed * factor[..., None] + jnp.einsum(
        "kgts,skd->kgtd",
        weights.astype(jnp.bfloat16),
        value_rows,
        preferred_element_type=jnp.float32,
    )
    return (new_peak, totals * factor + jnp.sum(weights, axis=-1), summed)


def backward_tile(
    carried, masked, query_tile, grad_tile, lse_tile, delta_tile, key_tile, value_tile, scaling
):
    grad_query, grad_key, grad_value = carried
    kv_local = query_tile.shape[1]
    key_rows = key_tile.reshape(key_tile.shape[0], kv_local, -1)
    value_rows = value_tile.reshape(value_tile.shape[0], kv_local, -1)
    scores = tile_scores(query_tile, key_rows, scaling)
    prob_tile = jnp.where(masked, jnp.exp(scores - lse_tile[..., None]), 0.0)
    grad_value = grad_value + jnp.einsum(
        "kgts,tkgd->skd",
        prob_tile.astype(jnp.bfloat16),
        grad_tile,
        preferred_element_type=jnp.float32,
    )
    dot_tile = jnp.einsum(
        "tkgd,skd->kgts", grad_tile, value_rows, preferred_element_type=jnp.float32
    )
    slopes = (prob_tile * (dot_tile - delta_tile[..., None])).astype(jnp.bfloat16)
    grad_query = grad_query + jnp.einsum(
        "kgts,skd->tkgd", slopes, key_rows, preferred_element_type=jnp.float32
    )
    grad_key = grad_key + jnp.einsum(
        "kgts,tkgd->skd", slopes, query_tile, preferred_element_type=jnp.float32
    )
    return (grad_query, grad_key, grad_value)


def anchors(member, cycle_size, counter):
    return ((member - counter) % cycle_size, (member - counter) % cycle_size)


def advance(current):
    return tuple(passed_along((current[0], current[1], current[2], current[3]), "outer", 1))


def rotate_grads(key_acc, value_acc):
    moved = (
        passed_along(key_acc.astype(jnp.bfloat16), "outer", 1).astype(key_acc.dtype),
        passed_along(value_acc.astype(jnp.bfloat16), "outer", 1).astype(value_acc.dtype),
    )
    return (moved[0], moved[1])


def on_device(
    queries, keys, values, grad_out, hidden_in, adapter_a, adapter_b, block_order, doc_ids
):
    cycle_size = lax.axis_size("outer")
    member = lax.axis_index("outer")
    tokens = queries.shape[0]
    half_rows = tokens // 2
    kv_local = keys.shape[1] // HEAD_DIM
    grp_local = queries.shape[1] // (kv_local * HEAD_DIM)
    scaling = HEAD_DIM ** (-0.5)
    query_rows = queries.reshape(tokens, kv_local, grp_local, HEAD_DIM)
    grad_rows = grad_out.reshape(tokens, kv_local, grp_local, HEAD_DIM)
    own_meta = joined_meta(
        block_meta(block_order, doc_ids, 2 * member, half_rows),
        block_meta(block_order, doc_ids, 2 * member + 1, half_rows),
    )
    local_keys = (keys[:half_rows], values[:half_rows], keys[half_rows:], values[half_rows:])
    low_partial = jnp.dot(hidden_in, adapter_a, preferred_element_type=jnp.float32)
    low_rank = lax.psum(low_partial, ("head", "inner")).astype(jnp.bfloat16)

    def sweep(counter, current, handle, carried):
        upper_src, lower_src = anchors(member, cycle_size, counter)
        key_meta = joined_meta(
            block_meta(block_order, doc_ids, 2 * upper_src, half_rows),
            block_meta(block_order, doc_ids, 2 * lower_src + 1, half_rows),
        )
        masked = visible(own_meta, key_meta)
        key_tile = jnp.concatenate((current[0], current[2]), 0)
        value_tile = jnp.concatenate((current[1], current[3]), 0)

        def active(present):
            return handle(present, masked, key_tile, value_tile)

        def resting(present):
            return present

        return lax.cond(jnp.any(masked), active, resting, carried)

    def forward_handle(present, masked, key_tile, value_tile):
        return forward_tile(present, masked, query_rows, key_tile, value_tile, scaling)

    start_state = (
        jnp.full((kv_local, grp_local, tokens), NEGATIVE, jnp.float32),
        jnp.zeros((kv_local, grp_local, tokens), jnp.float32),
        jnp.zeros((kv_local, grp_local, tokens, HEAD_DIM), jnp.float32),
    )

    def forward_turn(counter, loop_state):
        current, state = loop_state
        state = sweep(counter, current, forward_handle, state)
        return (advance(current), state)

    current, state = lax.fori_loop(0, cycle_size - 1, forward_turn, (local_keys, start_state))
    state = sweep(cycle_size - 1, current, forward_handle, state)
    peak_score, totals, summed = state
    lse_rows = peak_score + jnp.log(totals)
    output = summed / totals[..., None]
    delta_rows = jnp.sum(
        output * jnp.transpose(grad_rows, (1, 2, 0, 3)).astype(jnp.float32), axis=-1
    )
    empty_query = jnp.zeros((tokens, kv_local, grp_local, HEAD_DIM), jnp.float32)

    def backward_handle(present, masked, key_tile, value_tile):
        return backward_tile(
            present,
            masked,
            query_rows,
            grad_rows,
            lse_rows,
            delta_rows,
            key_tile,
            value_tile,
            scaling,
        )

    def backward_turn(counter, loop_state):
        current, carried = loop_state
        grad_query, key_acc, value_acc = sweep(counter, current, backward_handle, carried)
        key_acc, value_acc = rotate_grads(key_acc, value_acc)
        return (advance(current), (grad_query, key_acc, value_acc))

    empty_keys = jnp.zeros((tokens, kv_local, HEAD_DIM), jnp.float32)
    current, carried = lax.fori_loop(
        0, cycle_size - 1, backward_turn, (local_keys, (empty_query, empty_keys, empty_keys))
    )
    grad_queries, key_acc, value_acc = sweep(cycle_size - 1, current, backward_handle, carried)
    key_acc, value_acc = rotate_grads(key_acc, value_acc)
    key_acc, value_acc = (
        lax.psum(key_acc.astype(jnp.bfloat16), "inner").astype(jnp.float32),
        lax.psum(value_acc.astype(jnp.bfloat16), "inner").astype(jnp.float32),
    )
    grad_query = (grad_queries * scaling).astype(jnp.bfloat16).reshape(tokens, -1)
    grad_key = (key_acc * scaling).astype(jnp.bfloat16).reshape(tokens, -1)
    grad_value = value_acc.astype(jnp.bfloat16).reshape(tokens, -1)
    back_partial = lax.dot_general(
        grad_key, adapter_b, (((1,), (1,)), ((), ())), preferred_element_type=jnp.float32
    )
    back_rank = lax.psum(back_partial, "head").astype(jnp.bfloat16)
    grad_a_part = lax.dot_general(
        hidden_in, back_rank, (((0,), (0,)), ((), ())), preferred_element_type=jnp.float32
    )
    grad_b_part = lax.dot_general(
        low_rank, grad_key, (((0,), (0,)), ((), ())), preferred_element_type=jnp.float32
    )
    grad_a, grad_b = lax.psum((grad_a_part, grad_b_part), "outer")
    return (grad_query, grad_key, grad_value, grad_a, grad_b)


def solution(mesh):
    in_specs = (
        P("outer", ("head", "inner")),
        P("outer", "head"),
        P("outer", "head"),
        P("outer", ("head", "inner")),
        P("outer", ("head", "inner")),
        P(("head", "inner"), None),
        P(None, "head"),
        P(),
        P(),
    )
    out_specs = (
        P("outer", ("head", "inner")),
        P("outer", "head"),
        P("outer", "head"),
        P(("head", "inner"), None),
        P(None, "head"),
    )
    return jax.shard_map(
        on_device, mesh=mesh, in_specs=in_specs, out_specs=out_specs, check_vma=False
    )
```

profile of v0, /device:TPU:0, one launch (start us, length us, event | category | flops | bytes accessed | tf_op | source)
XLA Modules:
  0.0 191.0 jit_solution(2732203361276319303)
XLA Ops:
  14.9 30.7 %while.55 = (s32[]{:T(128)}, bf16[128,128]{1,0:T(8,128)(2,1)S(1)}, bf16[128,128]{1,0:T(8,128)(2,1)S(1)}, bf16[128,128]{1,0:T(8,128)(2,1)S(1)}, bf16[128,128]{1,0...) while((s32[]{:T(128)}, bf16[128,128]{1,0:T(8,128)(2,1)S(1)}, ...), condition=%wide.region_7.8_spmd, body=%wide.region_1.7_spmd.sunk | while | flops 68946208 | bytes 3714876 | solution.py:154
  14.9 3.1 %collective-permute-start = (bf16[128,128]{1,0:T(8,128)(2,1)S(1)}, bf16[128,128]{1,0:T(8,128)(2,1)S(1)}, u32[]{:S(2)}, u32[]{:S(2)}) collective-permute-start(bf16[128,128]{1,0:T(8,128)(2,1)S(1)} %copy.63), channel_id=1, source_target_pairs={{0,4},{4,8},{8,12},{12,0},{1,5},{5,9},{9,13},{13,1},{2,6},{6,10},{... | collective-permute-start | bytes 98312 | tf_op jit(solution)/shard_map/while/body/eval_jaxpr/ppermute | solution.py:13
  18.1 1.6 collective-permute-start.1
  19.6 1.6 collective-permute-start.2
  24.7 0.8 conditional.9
  25.6 1.3 collective-permute-done.3
  27.4 1.6 collective-permute-start.1
  29.0 1.6 collective-permute-start.2
  30.6 1.3 collective-permute-start.3
  33.9 0.8 fusion.112
  35.3 0.8 conditional.9
  36.8 1.6 collective-permute-start.1
  38.4 1.6 collective-permute-start.2
  39.9 1.3 collective-permute-start.3
  43.3 0.8 fusion.112
  44.7 0.8 conditional.9
  45.7 0.9 conditional.4
  46.7 50.4 %while.56 = (s32[]{:T(128)}, bf16[128,128]{1,0:T(8,128)(2,1)S(1)}, bf16[128,128]{1,0:T(8,128)(2,1)S(1)}, bf16[128,128]{1,0:T(8,128)(2,1)S(1)}, bf16[128,128]{1,0...) while((s32[]{:T(128)}, bf16[128,128]{1,0:T(8,128)(2,1)S(1)}, ...), condition=%wide.region_17.18_spmd.clone, body=%wide.region_13.0_spmd.clone.sunk | while | flops 169542432 | bytes 7159750 | solution.py:184
  50.3 1.3 conditional.10
  51.7 1.2 collective-permute-start.8
  52.9 1.6 collective-permute-start.4
  54.6 2.1 %collective-permute-start.5 = (bf16[128,128]{1,0:T(8,128)(2,1)S(1)}, bf16[128,128]{1,0:T(8,128)(2,1)S(1)}, u32[]{:S(2)}, u32[]{:S(2)}) collective-permute-start(bf16[128,128]{1,0:T(8,128)(2,1)S(1)} %copy.96), channel_id=1, source_target_pairs={{0,4},{4,8},{8,12},{12,0},{1,5},{5,9},{9,13},{13,1},{2,6},{6,10},{... | collective-permute-start | bytes 98312 | tf_op jit(solution)/shard_map/while/body/eval_jaxpr/ppermute | solution.py:13
  56.8 1.3 collective-permute-done.9
  59.1 1.1 collective-permute-done.5
  60.3 2.1 %collective-permute-done.6 = bf16[128,128]{1,0:T(8,128)(2,1)S(1)} collective-permute-done((bf16[128,128]{1,0:T(8,128)(2,1)S(1)}, bf16[128,128]{1,0:T(8,128)(2,1)S(1)}, u32[]{:S(2)}, u32[]{:S(2)}) %collective-permute-start.6) | collective-permute-done | bytes 32800 | tf_op jit(solution)/shard_map/while/body/eval_jaxpr/ppermute | solution.py:13
  62.4 1.4 collective-permute-done.7
  67.3 1.3 conditional.10
  68.8 1.7 collective-permute-start.4
  70.5 3.2 %collective-permute-start.5 = (bf16[128,128]{1,0:T(8,128)(2,1)S(1)}, bf16[128,128]{1,0:T(8,128)(2,1)S(1)}, u32[]{:S(2)}, u32[]{:S(2)}) collective-permute-start(bf16[128,128]{1,0:T(8,128)(2,1)S(1)} %copy.96), channel_id=1, source_target_pairs={{0,4},{4,8},{8,12},{12,0},{1,5},{5,9},{9,13},{13,1},{2,6},{6,10},{... | collective-permute-start | bytes 98312 | tf_op jit(solution)/shard_map/while/body/eval_jaxpr/ppermute | solution.py:13
  73.8 1.0 collective-permute-done.9
  76.2 3.2 %collective-permute-done.6 = bf16[128,128]{1,0:T(8,128)(2,1)S(1)} collective-permute-done((bf16[128,128]{1,0:T(8,128)(2,1)S(1)}, bf16[128,128]{1,0:T(8,128)(2,1)S(1)}, u32[]{:S(2)}, u32[]{:S(2)}) %collective-permute-start.6) | collective-permute-done | bytes 32800 | tf_op jit(solution)/shard_map/while/body/eval_jaxpr/ppermute | solution.py:13
  79.4 1.0 collective-permute-done.7
  84.0 1.3 conditional.10
  85.5 2.4 %collective-permute-start.4 = (bf16[128,128]{1,0:T(8,128)(2,1)S(1)}, bf16[128,128]{1,0:T(8,128)(2,1)S(1)}, u32[]{:S(2)}, u32[]{:S(2)}) collective-permute-start(bf16[128,128]{1,0:T(8,128)(2,1)S(1)} %copy.95), channel_id=1, source_target_pairs={{0,4},{4,8},{8,12},{12,0},{1,5},{5,9},{9,13},{13,1},{2,6},{6,10},{... | collective-permute-start | bytes 98312 | tf_op jit(solution)/shard_map/while/body/eval_jaxpr/ppermute | solution.py:13
  87.9 2.5 %collective-permute-start.5 = (bf16[128,128]{1,0:T(8,128)(2,1)S(1)}, bf16[128,128]{1,0:T(8,128)(2,1)S(1)}, u32[]{:S(2)}, u32[]{:S(2)}) collective-permute-start(bf16[128,128]{1,0:T(8,128)(2,1)S(1)} %copy.96), channel_id=1, source_target_pairs={{0,4},{4,8},{8,12},{12,0},{1,5},{5,9},{9,13},{13,1},{2,6},{6,10},{... | collective-permute-start | bytes 98312 | tf_op jit(solution)/shard_map/while/body/eval_jaxpr/ppermute | solution.py:13
  90.4 1.0 collective-permute-done.9
  92.6 1.3 collective-permute-done.5
  93.9 2.1 %collective-permute-done.6 = bf16[128,128]{1,0:T(8,128)(2,1)S(1)} collective-permute-done((bf16[128,128]{1,0:T(8,128)(2,1)S(1)}, bf16[128,128]{1,0:T(8,128)(2,1)S(1)}, u32[]{:S(2)}, u32[]{:S(2)}) %collective-permute-start.6) | collective-permute-done | bytes 32800 | tf_op jit(solution)/shard_map/while/body/eval_jaxpr/ppermute | solution.py:13
  96.1 1.0 collective-permute-done.7
  97.2 1.3 conditional.5
  99.5 5.0 %collective-permute-done.11 = bf16[256,1,128]{2,0,1:T(8,128)(2,1)S(1)} collective-permute-done((bf16[256,1,128]{2,0,1:T(8,128)(2,1)S(1)}, bf16[256,1,128]{2,0,1:T(8,128)(2,1)S(1)}, u32[]{:S(2)}, u32[]{:S(2)}) %collective-permute-start.11) | collective-permute-done | bytes 65568 | tf_op jit(solution)/shard_map/ppermute | solution.py:13
  106.8 23.6 %psum.46 = bf16[256,16]{1,0:T(8,128)(2,1)S(1)} all-reduce(f32[256,16]{1,0:T(8,128)S(1)} %fusion.90), channel_id=1, replica_groups=mesh['head'=2,'outer'=4,'inner'=4] {'head','inner'}, use_global_device_ids=true, to_apply=%region_24.25 | all-reduce | flops 4096 | bytes 24576 | tf_op jit(solution)/shard_map/psum | solution.py:120
  130.4 6.5 %all-reduce.6.cloned.1.call-done = (bf16[256,1,128]{2,0,1:T(8,128)(2,1)}, bf16[256,128]{1,0:T(8,128)(2,1)}) async-done(((bf16[256,1,128]{2,0,1:T(8,128)(2,1)}, bf16[256,128]{1,0:T(8,128)(2,1)}), (bf16[256,1,128]{2,0,1:T(8,128)(2,1)}, bf16[256,128]{1,0:T(8,128)(2,1)})) %all-reduce.6.cloned.1.call-update) | async-done | bytes 131088 | tf_op jit(solution)/shard_map/psum | solution.py:190
  136.9 0.9 fusion.71
  137.9 9.9 %psum.44 = bf16[256,16]{1,0:T(8,128)(2,1)S(1)} all-reduce(f32[256,16]{1,0:T(8,128)S(1)} %fusion.89), channel_id=1, replica_groups=mesh['head'=2,'outer'=4,'inner'=4] {'head'}, use_global_device_ids=true, to_apply=%region_22.23 | all-reduce | flops 4096 | bytes 24576 | tf_op jit(solution)/shard_map/psum | solution.py:199
  147.8 0.8 convolution_bitcast_fusion.10
  148.9 12.7 %psum.47 = f32[16,128]{1,0:T(8,128)} all-reduce(f32[16,128]{1,0:T(8,128)S(1)} %fusion.91), channel_id=1, replica_groups=mesh['head'=2,'outer'=4,'inner'=4] {'outer'}, use_global_device_ids=true, to_apply=%region_25.26 | all-reduce | flops 2048 | bytes 16384 | tf_op jit(solution)/shard_map/psum | solution.py:206
  161.6 21.1 %all-reduce.4.cloned.1.call-done = f32[1024,16]{0,1:T(8,128)} async-done(((f32[1024,16]{0,1:T(8,128)}), f32[1024,16]{0,1:T(8,128)}) %all-reduce.4.cloned.1.call-update) | async-done | bytes 65552 | tf_op jit(solution)/shard_map/psum | solution.py:206
  (230 shorter events, 30.4 us)
Async XLA Ops:
  7.2 91.4 %copy-start = (bf16[256,1024]{1,0:T(8,128)(2,1)S(1)}, bf16[256,1024]{1,0:T(8,128)(2,1)}, u32[]{:S(2)}) copy-start(bf16[256,1024]{1,0:T(8,128)(2,1)} %param.25) | copy-start | bytes 1572868
  7.2 129.7 %all-reduce.6.cloned.1.call-start = ((), (), s32[]{:S(2)}) async-start(), calls=%async_computation.1 | async-start | bytes 262144 | tf_op jit(solution)/shard_map/psum | solution.py:190
  7.3 4.0 %copy-start.11 = (s32[1024]{0:T(1024)S(1)}, s32[1024]{0:T(1024)}, u32[]{:S(2)}) copy-start(s32[1024]{0:T(1024)} %param.29) | copy-start | bytes 12292
  7.3 0.7 copy-start.2
  7.3 5.5 %copy-start.3 = (bf16[256,256]{1,0:T(8,128)(2,1)S(1)}, bf16[256,256]{1,0:T(8,128)(2,1)}, u32[]{:S(2)}) copy-start(bf16[256,256]{1,0:T(8,128)(2,1)} %param.21) | copy-start | bytes 393220
  12.9 0.9 copy-start.4
  13.9 0.8 copy-start.9
  13.9 0.9 copy-start.10
  14.9 10.6 %collective-permute-start = (bf16[128,128]{1,0:T(8,128)(2,1)S(1)}, bf16[128,128]{1,0:T(8,128)(2,1)S(1)}, u32[]{:S(2)}, u32[]{:S(2)}) collective-permute-start(bf16[128,128]{1,0:T(8,128)(2,1)S(1)} %copy.63), channel_id=1, source_target_pairs={{0,4},{4,8},{8,12},{12,0},{1,5},{5,9},{9,13},{13,1},{2,6},{6,10},{... | collective-permute-start | bytes 98312 | tf_op jit(solution)/shard_map/while/body/eval_jaxpr/ppermute | solution.py:13
  18.1 7.5 %collective-permute-start.1 = (bf16[128,128]{1,0:T(8,128)(2,1)S(1)}, bf16[128,128]{1,0:T(8,128)(2,1)S(1)}, u32[]{:S(2)}, u32[]{:S(2)}) collective-permute-start(bf16[128,128]{1,0:T(8,128)(2,1)S(1)} %copy.64), channel_id=1, source_target_pairs={{0,4},{4,8},{8,12},{12,0},{1,5},{5,9},{9,13},{13,1},{2,6},{6,10},{... | collective-permute-start | bytes 98312 | tf_op jit(solution)/shard_map/while/body/eval_jaxpr/ppermute | solution.py:13
  19.6 6.0 %collective-permute-start.2 = (bf16[128,128]{1,0:T(8,128)(2,1)S(1)}, bf16[128,128]{1,0:T(8,128)(2,1)S(1)}, u32[]{:S(2)}, u32[]{:S(2)}) collective-permute-start(bf16[128,128]{1,0:T(8,128)(2,1)S(1)} %copy.65), channel_id=1, source_target_pairs={{0,4},{4,8},{8,12},{12,0},{1,5},{5,9},{9,13},{13,1},{2,6},{6,10},{... | collective-permute-start | bytes 98312 | tf_op jit(solution)/shard_map/while/body/eval_jaxpr/ppermute | solution.py:13
  21.2 5.7 %collective-permute-start.3 = (bf16[128,128]{1,0:T(8,128)(2,1)S(1)}, bf16[128,128]{1,0:T(8,128)(2,1)S(1)}, u32[]{:S(2)}, u32[]{:S(2)}) collective-permute-start(bf16[128,128]{1,0:T(8,128)(2,1)S(1)} %copy.66), channel_id=1, source_target_pairs={{0,4},{4,8},{8,12},{12,0},{1,5},{5,9},{9,13},{13,1},{2,6},{6,10},{... | collective-permute-start | bytes 98312 | tf_op jit(solution)/shard_map/while/body/eval_jaxpr/ppermute | solution.py:13
  26.9 9.2 %collective-permute-start = (bf16[128,128]{1,0:T(8,128)(2,1)S(1)}, bf16[128,128]{1,0:T(8,128)(2,1)S(1)}, u32[]{:S(2)}, u32[]{:S(2)}) collective-permute-start(bf16[128,128]{1,0:T(8,128)(2,1)S(1)} %copy.63), channel_id=1, source_target_pairs={{0,4},{4,8},{8,12},{12,0},{1,5},{5,9},{9,13},{13,1},{2,6},{6,10},{... | collective-permute-start | bytes 98312 | tf_op jit(solution)/shard_map/while/body/eval_jaxpr/ppermute | solution.py:13
  27.4 8.8 %collective-permute-start.1 = (bf16[128,128]{1,0:T(8,128)(2,1)S(1)}, bf16[128,128]{1,0:T(8,128)(2,1)S(1)}, u32[]{:S(2)}, u32[]{:S(2)}) collective-permute-start(bf16[128,128]{1,0:T(8,128)(2,1)S(1)} %copy.64), channel_id=1, source_target_pairs={{0,4},{4,8},{8,12},{12,0},{1,5},{5,9},{9,13},{13,1},{2,6},{6,10},{... | collective-permute-start | bytes 98312 | tf_op jit(solution)/shard_map/while/body/eval_jaxpr/ppermute | solution.py:13
  29.0 7.2 %collective-permute-start.2 = (bf16[128,128]{1,0:T(8,128)(2,1)S(1)}, bf16[128,128]{1,0:T(8,128)(2,1)S(1)}, u32[]{:S(2)}, u32[]{:S(2)}) collective-permute-start(bf16[128,128]{1,0:T(8,128)(2,1)S(1)} %copy.65), channel_id=1, source_target_pairs={{0,4},{4,8},{8,12},{12,0},{1,5},{5,9},{9,13},{13,1},{2,6},{6,10},{... | collective-permute-start | bytes 98312 | tf_op jit(solution)/shard_map/while/body/eval_jaxpr/ppermute | solution.py:13
  30.6 5.7 %collective-permute-start.3 = (bf16[128,128]{1,0:T(8,128)(2,1)S(1)}, bf16[128,128]{1,0:T(8,128)(2,1)S(1)}, u32[]{:S(2)}, u32[]{:S(2)}) collective-permute-start(bf16[128,128]{1,0:T(8,128)(2,1)S(1)} %copy.66), channel_id=1, source_target_pairs={{0,4},{4,8},{8,12},{12,0},{1,5},{5,9},{9,13},{13,1},{2,6},{6,10},{... | collective-permute-start | bytes 98312 | tf_op jit(solution)/shard_map/while/body/eval_jaxpr/ppermute | solution.py:13
  36.3 9.2 %collective-permute-start = (bf16[128,128]{1,0:T(8,128)(2,1)S(1)}, bf16[128,128]{1,0:T(8,128)(2,1)S(1)}, u32[]{:S(2)}, u32[]{:S(2)}) collective-permute-start(bf16[128,128]{1,0:T(8,128)(2,1)S(1)} %copy.63), channel_id=1, source_target_pairs={{0,4},{4,8},{8,12},{12,0},{1,5},{5,9},{9,13},{13,1},{2,6},{6,10},{... | collective-permute-start | bytes 98312 | tf_op jit(solution)/shard_map/while/body/eval_jaxpr/ppermute | solution.py:13
  36.8 8.8 %collective-permute-start.1 = (bf16[128,128]{1,0:T(8,128)(2,1)S(1)}, bf16[128,128]{1,0:T(8,128)(2,1)S(1)}, u32[]{:S(2)}, u32[]{:S(2)}) collective-permute-start(bf16[128,128]{1,0:T(8,128)(2,1)S(1)} %copy.64), channel_id=1, source_target_pairs={{0,4},{4,8},{8,12},{12,0},{1,5},{5,9},{9,13},{13,1},{2,6},{6,10},{... | collective-permute-start | bytes 98312 | tf_op jit(solution)/shard_map/while/body/eval_jaxpr/ppermute | solution.py:13
  38.4 7.2 %collective-permute-start.2 = (bf16[128,128]{1,0:T(8,128)(2,1)S(1)}, bf16[128,128]{1,0:T(8,128)(2,1)S(1)}, u32[]{:S(2)}, u32[]{:S(2)}) collective-permute-start(bf16[128,128]{1,0:T(8,128)(2,1)S(1)} %copy.65), channel_id=1, source_target_pairs={{0,4},{4,8},{8,12},{12,0},{1,5},{5,9},{9,13},{13,1},{2,6},{6,10},{... | collective-permute-start | bytes 98312 | tf_op jit(solution)/shard_map/while/body/eval_jaxpr/ppermute | solution.py:13
  39.9 5.7 %collective-permute-start.3 = (bf16[128,128]{1,0:T(8,128)(2,1)S(1)}, bf16[128,128]{1,0:T(8,128)(2,1)S(1)}, u32[]{:S(2)}, u32[]{:S(2)}) collective-permute-start(bf16[128,128]{1,0:T(8,128)(2,1)S(1)} %copy.66), channel_id=1, source_target_pairs={{0,4},{4,8},{8,12},{12,0},{1,5},{5,9},{9,13},{13,1},{2,6},{6,10},{... | collective-permute-start | bytes 98312 | tf_op jit(solution)/shard_map/while/body/eval_jaxpr/ppermute | solution.py:13
  51.6 6.5 %collective-permute-start.9 = (bf16[256,1,128]{2,0,1:T(8,128)(2,1)S(1)}, bf16[256,1,128]{2,0,1:T(8,128)(2,1)S(1)}, u32[]{:S(2)}, u32[]{:S(2)}) collective-permute-start(bf16[256,1,128]{2,0,1:T(8,128)(2,1)S(1)} %convert_element_type.175), channel_id=1, source_target_pairs={{0,4},{4,8},{8,12},{12,0},{1,5},{5,9},{9,13},{13,1},{2,6},{6,10},{... | collective-permute-start | bytes 196616 | tf_op jit(solution)/shard_map/while/body/eval_jaxpr/ppermute | solution.py:13
  51.7 7.1 %collective-permute-start.8 = (bf16[256,1,128]{2,0,1:T(8,128)(2,1)S(1)}, bf16[256,1,128]{2,0,1:T(8,128)(2,1)S(1)}, u32[]{:S(2)}, u32[]{:S(2)}) collective-permute-start(bf16[256,1,128]{2,0,1:T(8,128)(2,1)S(1)} %convert_element_type.173), channel_id=1, source_target_pairs={{0,4},{4,8},{8,12},{12,0},{1,5},{5,9},{9,13},{13,1},{2,6},{6,10},{... | collective-permute-start | bytes 196616 | tf_op jit(solution)/shard_map/while/body/eval_jaxpr/ppermute | solution.py:13
  52.9 6.2 %collective-permute-start.4 = (bf16[128,128]{1,0:T(8,128)(2,1)S(1)}, bf16[128,128]{1,0:T(8,128)(2,1)S(1)}, u32[]{:S(2)}, u32[]{:S(2)}) collective-permute-start(bf16[128,128]{1,0:T(8,128)(2,1)S(1)} %copy.95), channel_id=1, source_target_pairs={{0,4},{4,8},{8,12},{12,0},{1,5},{5,9},{9,13},{13,1},{2,6},{6,10},{... | collective-permute-start | bytes 98312 | tf_op jit(solution)/shard_map/while/body/eval_jaxpr/ppermute | solution.py:13
  54.6 5.7 %collective-permute-start.5 = (bf16[128,128]{1,0:T(8,128)(2,1)S(1)}, bf16[128,128]{1,0:T(8,128)(2,1)S(1)}, u32[]{:S(2)}, u32[]{:S(2)}) collective-permute-start(bf16[128,128]{1,0:T(8,128)(2,1)S(1)} %copy.96), channel_id=1, source_target_pairs={{0,4},{4,8},{8,12},{12,0},{1,5},{5,9},{9,13},{13,1},{2,6},{6,10},{... | collective-permute-start | bytes 98312 | tf_op jit(solution)/shard_map/while/body/eval_jaxpr/ppermute | solution.py:13
  56.7 5.7 %collective-permute-start.6 = (bf16[128,128]{1,0:T(8,128)(2,1)S(1)}, bf16[128,128]{1,0:T(8,128)(2,1)S(1)}, u32[]{:S(2)}, u32[]{:S(2)}) collective-permute-start(bf16[128,128]{1,0:T(8,128)(2,1)S(1)} %copy.97), channel_id=1, source_target_pairs={{0,4},{4,8},{8,12},{12,0},{1,5},{5,9},{9,13},{13,1},{2,6},{6,10},{... | collective-permute-start | bytes 98312 | tf_op jit(solution)/shard_map/while/body/eval_jaxpr/ppermute | solution.py:13
  58.1 5.7 %collective-permute-start.7 = (bf16[128,128]{1,0:T(8,128)(2,1)S(1)}, bf16[128,128]{1,0:T(8,128)(2,1)S(1)}, u32[]{:S(2)}, u32[]{:S(2)}) collective-permute-start(bf16[128,128]{1,0:T(8,128)(2,1)S(1)} %copy.98), channel_id=1, source_target_pairs={{0,4},{4,8},{8,12},{12,0},{1,5},{5,9},{9,13},{13,1},{2,6},{6,10},{... | collective-permute-start | bytes 98312 | tf_op jit(solution)/shard_map/while/body/eval_jaxpr/ppermute | solution.py:13
  68.6 6.1 %collective-permute-start.9 = (bf16[256,1,128]{2,0,1:T(8,128)(2,1)S(1)}, bf16[256,1,128]{2,0,1:T(8,128)(2,1)S(1)}, u32[]{:S(2)}, u32[]{:S(2)}) collective-permute-start(bf16[256,1,128]{2,0,1:T(8,128)(2,1)S(1)} %convert_element_type.175), channel_id=1, source_target_pairs={{0,4},{4,8},{8,12},{12,0},{1,5},{5,9},{9,13},{13,1},{2,6},{6,10},{... | collective-permute-start | bytes 196616 | tf_op jit(solution)/shard_map/while/body/eval_jaxpr/ppermute | solution.py:13
  68.7 6.7 %collective-permute-start.8 = (bf16[256,1,128]{2,0,1:T(8,128)(2,1)S(1)}, bf16[256,1,128]{2,0,1:T(8,128)(2,1)S(1)}, u32[]{:S(2)}, u32[]{:S(2)}) collective-permute-start(bf16[256,1,128]{2,0,1:T(8,128)(2,1)S(1)} %convert_element_type.173), channel_id=1, source_target_pairs={{0,4},{4,8},{8,12},{12,0},{1,5},{5,9},{9,13},{13,1},{2,6},{6,10},{... | collective-permute-start | bytes 196616 | tf_op jit(solution)/shard_map/while/body/eval_jaxpr/ppermute | solution.py:13
  68.8 7.0 %collective-permute-start.4 = (bf16[128,128]{1,0:T(8,128)(2,1)S(1)}, bf16[128,128]{1,0:T(8,128)(2,1)S(1)}, u32[]{:S(2)}, u32[]{:S(2)}) collective-permute-start(bf16[128,128]{1,0:T(8,128)(2,1)S(1)} %copy.95), channel_id=1, source_target_pairs={{0,4},{4,8},{8,12},{12,0},{1,5},{5,9},{9,13},{13,1},{2,6},{6,10},{... | collective-permute-start | bytes 98312 | tf_op jit(solution)/shard_map/while/body/eval_jaxpr/ppermute | solution.py:13
  70.5 5.7 %collective-permute-start.5 = (bf16[128,128]{1,0:T(8,128)(2,1)S(1)}, bf16[128,128]{1,0:T(8,128)(2,1)S(1)}, u32[]{:S(2)}, u32[]{:S(2)}) collective-permute-start(bf16[128,128]{1,0:T(8,128)(2,1)S(1)} %copy.96), channel_id=1, source_target_pairs={{0,4},{4,8},{8,12},{12,0},{1,5},{5,9},{9,13},{13,1},{2,6},{6,10},{... | collective-permute-start | bytes 98312 | tf_op jit(solution)/shard_map/while/body/eval_jaxpr/ppermute | solution.py:13
  73.7 5.7 %collective-permute-start.6 = (bf16[128,128]{1,0:T(8,128)(2,1)S(1)}, bf16[128,128]{1,0:T(8,128)(2,1)S(1)}, u32[]{:S(2)}, u32[]{:S(2)}) collective-permute-start(bf16[128,128]{1,0:T(8,128)(2,1)S(1)} %copy.97), channel_id=1, source_target_pairs={{0,4},{4,8},{8,12},{12,0},{1,5},{5,9},{9,13},{13,1},{2,6},{6,10},{... | collective-permute-start | bytes 98312 | tf_op jit(solution)/shard_map/while/body/eval_jaxpr/ppermute | solution.py:13
  74.8 5.7 %collective-permute-start.7 = (bf16[128,128]{1,0:T(8,128)(2,1)S(1)}, bf16[128,128]{1,0:T(8,128)(2,1)S(1)}, u32[]{:S(2)}, u32[]{:S(2)}) collective-permute-start(bf16[128,128]{1,0:T(8,128)(2,1)S(1)} %copy.98), channel_id=1, source_target_pairs={{0,4},{4,8},{8,12},{12,0},{1,5},{5,9},{9,13},{13,1},{2,6},{6,10},{... | collective-permute-start | bytes 98312 | tf_op jit(solution)/shard_map/while/body/eval_jaxpr/ppermute | solution.py:13
  85.3 6.1 %collective-permute-start.9 = (bf16[256,1,128]{2,0,1:T(8,128)(2,1)S(1)}, bf16[256,1,128]{2,0,1:T(8,128)(2,1)S(1)}, u32[]{:S(2)}, u32[]{:S(2)}) collective-permute-start(bf16[256,1,128]{2,0,1:T(8,128)(2,1)S(1)} %convert_element_type.175), channel_id=1, source_target_pairs={{0,4},{4,8},{8,12},{12,0},{1,5},{5,9},{9,13},{13,1},{2,6},{6,10},{... | collective-permute-start | bytes 196616 | tf_op jit(solution)/shard_map/while/body/eval_jaxpr/ppermute | solution.py:13
  85.4 6.7 %collective-permute-start.8 = (bf16[256,1,128]{2,0,1:T(8,128)(2,1)S(1)}, bf16[256,1,128]{2,0,1:T(8,128)(2,1)S(1)}, u32[]{:S(2)}, u32[]{:S(2)}) collective-permute-start(bf16[256,1,128]{2,0,1:T(8,128)(2,1)S(1)} %convert_element_type.173), channel_id=1, source_target_pairs={{0,4},{4,8},{8,12},{12,0},{1,5},{5,9},{9,13},{13,1},{2,6},{6,10},{... | collective-permute-start | bytes 196616 | tf_op jit(solution)/shard_map/while/body/eval_jaxpr/ppermute | solution.py:13
  85.5 7.2 %collective-permute-start.4 = (bf16[128,128]{1,0:T(8,128)(2,1)S(1)}, bf16[128,128]{1,0:T(8,128)(2,1)S(1)}, u32[]{:S(2)}, u32[]{:S(2)}) collective-permute-start(bf16[128,128]{1,0:T(8,128)(2,1)S(1)} %copy.95), channel_id=1, source_target_pairs={{0,4},{4,8},{8,12},{12,0},{1,5},{5,9},{9,13},{13,1},{2,6},{6,10},{... | collective-permute-start | bytes 98312 | tf_op jit(solution)/shard_map/while/body/eval_jaxpr/ppermute | solution.py:13
  87.9 6.1 %collective-permute-start.5 = (bf16[128,128]{1,0:T(8,128)(2,1)S(1)}, bf16[128,128]{1,0:T(8,128)(2,1)S(1)}, u32[]{:S(2)}, u32[]{:S(2)}) collective-permute-start(bf16[128,128]{1,0:T(8,128)(2,1)S(1)} %copy.96), channel_id=1, source_target_pairs={{0,4},{4,8},{8,12},{12,0},{1,5},{5,9},{9,13},{13,1},{2,6},{6,10},{... | collective-permute-start | bytes 98312 | tf_op jit(solution)/shard_map/while/body/eval_jaxpr/ppermute | solution.py:13
  90.4 5.7 %collective-permute-start.6 = (bf16[128,128]{1,0:T(8,128)(2,1)S(1)}, bf16[128,128]{1,0:T(8,128)(2,1)S(1)}, u32[]{:S(2)}, u32[]{:S(2)}) collective-permute-start(bf16[128,128]{1,0:T(8,128)(2,1)S(1)} %copy.97), channel_id=1, source_target_pairs={{0,4},{4,8},{8,12},{12,0},{1,5},{5,9},{9,13},{13,1},{2,6},{6,10},{... | collective-permute-start | bytes 98312 | tf_op jit(solution)/shard_map/while/body/eval_jaxpr/ppermute | solution.py:13
  91.4 5.7 %collective-permute-start.7 = (bf16[128,128]{1,0:T(8,128)(2,1)S(1)}, bf16[128,128]{1,0:T(8,128)(2,1)S(1)}, u32[]{:S(2)}, u32[]{:S(2)}) collective-permute-start(bf16[128,128]{1,0:T(8,128)(2,1)S(1)} %copy.98), channel_id=1, source_target_pairs={{0,4},{4,8},{8,12},{12,0},{1,5},{5,9},{9,13},{13,1},{2,6},{6,10},{... | collective-permute-start | bytes 98312 | tf_op jit(solution)/shard_map/while/body/eval_jaxpr/ppermute | solution.py:13
  98.4 6.1 %collective-permute-start.11 = (bf16[256,1,128]{2,0,1:T(8,128)(2,1)S(1)}, bf16[256,1,128]{2,0,1:T(8,128)(2,1)S(1)}, u32[]{:S(2)}, u32[]{:S(2)}) collective-permute-start(bf16[256,1,128]{2,0,1:T(8,128)(2,1)S(1)} %convert_element_type.122), channel_id=1, source_target_pairs={{0,4},{4,8},{8,12},{12,0},{1,5},{5,9},{9,13},{13,1},{2,6},{6,10},{... | collective-permute-start | bytes 196616 | tf_op jit(solution)/shard_map/ppermute | solution.py:13
  98.5 0.8 copy-start.12
  98.5 6.7 %collective-permute-start.10 = (bf16[256,1,128]{2,0,1:T(8,128)(2,1)S(1)}, bf16[256,1,128]{2,0,1:T(8,128)(2,1)S(1)}, u32[]{:S(2)}, u32[]{:S(2)}) collective-permute-start(bf16[256,1,128]{2,0,1:T(8,128)(2,1)S(1)} %convert_element_type.119), channel_id=1, source_target_pairs={{0,4},{4,8},{8,12},{12,0},{1,5},{5,9},{9,13},{13,1},{2,6},{6,10},{... | collective-permute-start | bytes 196616 | tf_op jit(solution)/shard_map/ppermute | solution.py:13
  104.5 0.7 copy-start.6
  105.2 0.6 copy-start.7
  105.9 76.8 %all-reduce.4.cloned.1.call-start = ((), (), s32[]{:S(2)}) async-start(), calls=%async_computation | async-start | bytes 131072 | tf_op jit(solution)/shard_map/psum | solution.py:206
  136.9 0.9 copy-start.13
  137.8 10.9 %copy-start.1 = (bf16[256,128]{1,0:T(8,128)(2,1)}, bf16[256,128]{1,0:T(8,128)(2,1)S(1)}, u32[]{:S(2)}) copy-start(bf16[256,128]{1,0:T(8,128)(2,1)S(1)} %fusion.71) | copy-start | bytes 196612
  148.7 34.0 %copy-start.5 = (bf16[256,128]{1,0:T(8,128)(2,1)S(1)}, bf16[256,128]{1,0:T(8,128)(2,1)}, u32[]{:S(2)}) copy-start(bf16[256,128]{1,0:T(8,128)(2,1)} %get-tuple-element.1577) | copy-start | bytes 196612
  182.7 0.9 copy-start.8
Sparse Core Ops, SparseCore 0:
  106.0 30.8 all-reduce.5
  148.8 33.8 all-reduce.3
where the time goes:
time: 192 us; the launch traced here: 191 us
  waiting for transfers between devices  55.2 us (29%)
  blocking collectives  46.2 us (24%)
  starting transfers between devices  31.7 us (17%)
  between operations  17.7 us (9%)
  loops' own time  12.8 us (7%)
  local copies, waits for them, and re-layouts  11.2 us (6%)
  matrix products  8.69 us (5%)
  other arithmetic  7.44 us (4%)
    ppermute x32, starting transfers between devices, passed_along(): return lax.ppermute(value, axis, pairs)  31.7 us
    ppermute x32, waiting for transfers between devices, passed_along(): return lax.ppermute(value, axis, pairs)  27.6 us
    psum x1, blocking collectives, on_device(): low_rank = lax.psum(low_partial, ('head', 'inner')).astype(jnp.bfloat16)  23.6 us
    psum x1, waiting for transfers between devices, on_device(): grad_a, grad_b = lax.psum((grad_a_part, grad_b_part), 'outer')  21.1 us
    psum x1, blocking collectives, on_device(): grad_a, grad_b = lax.psum((grad_a_part, grad_b_part), 'outer')  12.7 us
    psum x1, blocking collectives, on_device(): back_rank = lax.psum(back_partial, 'head').astype(jnp.bfloat16)  9.87 us
    psum x1, waiting for transfers between devices, on_device(): lax.psum(key_acc.astype(jnp.bfloat16), 'inner').astype(jnp.float32)  6.49 us
    another operation x1, loops' own time, on_device(): lax.fori_loop(0, cycle_size - 1, backward_turn, (local_keys, (empty_query...  6.29 us
  transfers between devices with their start and end apart: 34, of which 25 were waited for; matrix products, arithmetic and copies ran while one was open for 4% of the time, Pallas kernels for 0%

commit v1 on v0

--- a/solution.py
+++ b/solution.py
@@ -117,7 +117,7 @@
     )
     local_keys = (keys[:half_rows], values[:half_rows], keys[half_rows:], values[half_rows:])
     low_partial = jnp.dot(hidden_in, adapter_a, preferred_element_type=jnp.float32)
-    low_rank = lax.psum(low_partial, ("head", "inner")).astype(jnp.bfloat16)
+    low_rank = lax.psum(lax.psum(low_partial, "head"), "inner").astype(jnp.bfloat16)
 
     def sweep(counter, current, handle, carried):
         upper_src, lower_src = anchors(member, cycle_size, counter)

time: 192 us -> 206 us (1.073)
  waiting for transfers between devices: 55.2 us -> 78.7 us
  blocking collectives: 46.2 us -> 36.3 us
    psum x1, waiting for transfers between devices: 6.49 us -> 30.1 us  [on_device(): lax.psum(key_acc.astype(jnp.bfloat16), 'inner').astype(jnp.float32)]
    psum x1, blocking collectives: 23.6 us -> 11.7 us  [on_device(): lax.psum(lax.psum(low_partial, 'head'), 'inner').astype(jnp.bfloat16)]
    psum x1, blocking collectives: 9.87 us -> 12.4 us  [on_device(): back_rank = lax.psum(back_partial, 'head').astype(jnp.bfloat16)]
    unnamed x39 -> x35, local copies, waits for them, and re-layouts: 6.13 us -> 6.14 us
where the time goes in v1:
time: 206 us; the launch traced here: 205 us
  waiting for transfers between devices  78.7 us (38%)
  blocking collectives  36.3 us (18%)
  starting transfers between devices  31.8 us (15%)
  between operations  17.7 us (9%)
  loops' own time  12.8 us (6%)
  local copies, waits for them, and re-layouts  12.1 us (6%)
  matrix products  8.7 us (4%)
  other arithmetic  7.44 us (4%)
    ppermute x32, starting transfers between devices, passed_along(): return lax.ppermute(value, axis, pairs)  31.7 us
    psum x1, waiting for transfers between devices, on_device(): lax.psum(key_acc.astype(jnp.bfloat16), 'inner').astype(jnp.float32)  30.1 us
    ppermute x32, waiting for transfers between devices, passed_along(): return lax.ppermute(value, axis, pairs)  27.6 us
    psum x1, waiting for transfers between devices, on_device(): grad_a, grad_b = lax.psum((grad_a_part, grad_b_part), 'outer')  21 us
    psum x1, blocking collectives, on_device(): back_rank = lax.psum(back_partial, 'head').astype(jnp.bfloat16)  12.4 us
    psum x1, blocking collectives, on_device(): grad_a, grad_b = lax.psum((grad_a_part, grad_b_part), 'outer')  12.2 us
    psum x1, blocking collectives, on_device(): lax.psum(lax.psum(low_partial, 'head'), 'inner').astype(jnp.bfloat16)  11.7 us
    another operation x1, loops' own time, on_device(): lax.fori_loop(0, cycle_size - 1, backward_turn, (local_keys, (empty_query...  6.31 us
  transfers between devices with their start and end apart: 34, of which 25 were waited for; matrix products, arithmetic and copies ran while one was open for 4% of the time, Pallas kernels for 0%

profile of v1, /device:TPU:0, one launch (start us, length us, event | category | flops | bytes accessed | tf_op | source)
XLA Modules:
  0.0 205.4 jit_solution(12089945055986489718)
XLA Ops:
  11.2 0.8 fusion.85
  12.1 0.8 copy-done.3
  15.7 30.7 %while.55 = (s32[]{:T(128)}, bf16[128,128]{1,0:T(8,128)(2,1)S(1)}, bf16[128,128]{1,0:T(8,128)(2,1)S(1)}, bf16[128,128]{1,0:T(8,128)(2,1)S(1)}, bf16[128,128]{1,0...) while((s32[]{:T(128)}, bf16[128,128]{1,0:T(8,128)(2,1)S(1)}, ...), condition=%wide.region_7.8_spmd, body=%wide.region_1.7_spmd.sunk | while | flops 68946208 | bytes 3714876 | solution.py:154
  15.7 3.1 %collective-permute-start = (bf16[128,128]{1,0:T(8,128)(2,1)S(1)}, bf16[128,128]{1,0:T(8,128)(2,1)S(1)}, u32[]{:S(2)}, u32[]{:S(2)}) collective-permute-start(bf16[128,128]{1,0:T(8,128)(2,1)S(1)} %copy.63), channel_id=1, source_target_pairs={{0,4},{4,8},{8,12},{12,0},{1,5},{5,9},{9,13},{13,1},{2,6},{6,10},{... | collective-permute-start | bytes 98312 | tf_op jit(solution)/shard_map/while/body/eval_jaxpr/ppermute | solution.py:13
  18.8 1.6 collective-permute-start.1
  20.4 1.6 collective-permute-start.2
  25.5 0.8 conditional.9
  26.4 1.3 collective-permute-done.3
  28.2 1.6 collective-permute-start.1
  29.8 1.6 collective-permute-start.2
  31.4 1.3 collective-permute-start.3
  36.1 0.8 conditional.9
  37.6 1.6 collective-permute-start.1
  39.2 1.6 collective-permute-start.2
  40.7 1.3 collective-permute-start.3
  45.5 0.8 conditional.9
  46.5 0.9 conditional.4
  47.5 50.4 %while.56 = (s32[]{:T(128)}, bf16[128,128]{1,0:T(8,128)(2,1)S(1)}, bf16[128,128]{1,0:T(8,128)(2,1)S(1)}, bf16[128,128]{1,0:T(8,128)(2,1)S(1)}, bf16[128,128]{1,0...) while((s32[]{:T(128)}, bf16[128,128]{1,0:T(8,128)(2,1)S(1)}, ...), condition=%wide.region_17.18_spmd.clone, body=%wide.region_13.17_spmd.clone.sunk | while | flops 169542432 | bytes 7159750 | solution.py:184
  51.1 1.3 conditional.10
  52.5 1.2 collective-permute-start.9
  53.7 1.6 collective-permute-start.4
  55.3 2.1 %collective-permute-start.5 = (bf16[128,128]{1,0:T(8,128)(2,1)S(1)}, bf16[128,128]{1,0:T(8,128)(2,1)S(1)}, u32[]{:S(2)}, u32[]{:S(2)}) collective-permute-start(bf16[128,128]{1,0:T(8,128)(2,1)S(1)} %copy.96), channel_id=1, source_target_pairs={{0,4},{4,8},{8,12},{12,0},{1,5},{5,9},{9,13},{13,1},{2,6},{6,10},{... | collective-permute-start | bytes 98312 | tf_op jit(solution)/shard_map/while/body/eval_jaxpr/ppermute | solution.py:13
  57.5 1.3 collective-permute-done.8
  59.9 1.1 collective-permute-done.5
  61.1 2.1 %collective-permute-done.6 = bf16[128,128]{1,0:T(8,128)(2,1)S(1)} collective-permute-done((bf16[128,128]{1,0:T(8,128)(2,1)S(1)}, bf16[128,128]{1,0:T(8,128)(2,1)S(1)}, u32[]{:S(2)}, u32[]{:S(2)}) %collective-permute-start.6) | collective-permute-done | bytes 32800 | tf_op jit(solution)/shard_map/while/body/eval_jaxpr/ppermute | solution.py:13
  63.2 1.4 collective-permute-done.7
  68.1 1.3 conditional.10
  69.6 1.7 collective-permute-start.4
  71.3 3.2 %collective-permute-start.5 = (bf16[128,128]{1,0:T(8,128)(2,1)S(1)}, bf16[128,128]{1,0:T(8,128)(2,1)S(1)}, u32[]{:S(2)}, u32[]{:S(2)}) collective-permute-start(bf16[128,128]{1,0:T(8,128)(2,1)S(1)} %copy.96), channel_id=1, source_target_pairs={{0,4},{4,8},{8,12},{12,0},{1,5},{5,9},{9,13},{13,1},{2,6},{6,10},{... | collective-permute-start | bytes 98312 | tf_op jit(solution)/shard_map/while/body/eval_jaxpr/ppermute | solution.py:13
  74.6 1.0 collective-permute-done.8
  77.0 3.2 %collective-permute-done.6 = bf16[128,128]{1,0:T(8,128)(2,1)S(1)} collective-permute-done((bf16[128,128]{1,0:T(8,128)(2,1)S(1)}, bf16[128,128]{1,0:T(8,128)(2,1)S(1)}, u32[]{:S(2)}, u32[]{:S(2)}) %collective-permute-start.6) | collective-permute-done | bytes 32800 | tf_op jit(solution)/shard_map/while/body/eval_jaxpr/ppermute | solution.py:13
  80.2 1.0 collective-permute-done.7
  84.8 1.3 conditional.10
  86.3 2.4 %collective-permute-start.4 = (bf16[128,128]{1,0:T(8,128)(2,1)S(1)}, bf16[128,128]{1,0:T(8,128)(2,1)S(1)}, u32[]{:S(2)}, u32[]{:S(2)}) collective-permute-start(bf16[128,128]{1,0:T(8,128)(2,1)S(1)} %copy.95), channel_id=1, source_target_pairs={{0,4},{4,8},{8,12},{12,0},{1,5},{5,9},{9,13},{13,1},{2,6},{6,10},{... | collective-permute-start | bytes 98312 | tf_op jit(solution)/shard_map/while/body/eval_jaxpr/ppermute | solution.py:13
  88.7 2.5 %collective-permute-start.5 = (bf16[128,128]{1,0:T(8,128)(2,1)S(1)}, bf16[128,128]{1,0:T(8,128)(2,1)S(1)}, u32[]{:S(2)}, u32[]{:S(2)}) collective-permute-start(bf16[128,128]{1,0:T(8,128)(2,1)S(1)} %copy.96), channel_id=1, source_target_pairs={{0,4},{4,8},{8,12},{12,0},{1,5},{5,9},{9,13},{13,1},{2,6},{6,10},{... | collective-permute-start | bytes 98312 | tf_op jit(solution)/shard_map/while/body/eval_jaxpr/ppermute | solution.py:13
  91.2 1.0 collective-permute-done.8
  93.4 1.3 collective-permute-done.5
  94.7 2.1 %collective-permute-done.6 = bf16[128,128]{1,0:T(8,128)(2,1)S(1)} collective-permute-done((bf16[128,128]{1,0:T(8,128)(2,1)S(1)}, bf16[128,128]{1,0:T(8,128)(2,1)S(1)}, u32[]{:S(2)}, u32[]{:S(2)}) %collective-permute-start.6) | collective-permute-done | bytes 32800 | tf_op jit(solution)/shard_map/while/body/eval_jaxpr/ppermute | solution.py:13
  96.9 1.0 collective-permute-done.7
  98.0 1.2 conditional.5
  100.3 5.0 %collective-permute-done.11 = bf16[256,1,128]{2,0,1:T(8,128)(2,1)S(1)} collective-permute-done((bf16[256,1,128]{2,0,1:T(8,128)(2,1)S(1)}, bf16[256,1,128]{2,0,1:T(8,128)(2,1)S(1)}, u32[]{:S(2)}, u32[]{:S(2)}) %collective-permute-start.11) | collective-permute-done | bytes 65568 | tf_op jit(solution)/shard_map/ppermute | solution.py:13
  107.6 30.1 %all-reduce.7.cloned.1.call-done = (bf16[256,1,128]{2,0,1:T(8,128)(2,1)}, bf16[256,128]{1,0:T(8,128)(2,1)}) async-done(((bf16[256,1,128]{2,0,1:T(8,128)(2,1)}, bf16[256,128]{1,0:T(8,128)(2,1)}), (bf16[256,1,128]{2,0,1:T(8,128)(2,1)}, bf16[256,128]{1,0:T(8,128)(2,1)})) %all-reduce.7.cloned.1.call-update) | async-done | bytes 131088 | tf_op jit(solution)/shard_map/psum | solution.py:190
  137.8 0.9 fusion.71
  138.8 12.4 %all-reduce = (bf16[256,16]{1,0:T(8,128)(2,1)S(1)}, f32[256,16]{1,0:T(8,128)S(1)}) all-reduce(f32[256,16]{1,0:T(8,128)S(1)} %fusion.89, f32[256,16]{1,0:T(8,128)S(1)} %fusion.90), channel_id=1, replica_groups=mesh['head'=2,'outer'=4,'inner'=4] {'head'}, use_global_device_ids=true, to_apply=%region_22.23 | all-reduce | flops 8192 | bytes 57344 | tf_op jit(solution)/shard_map/psum | solution.py:199
  151.2 11.7 %psum.54 = bf16[256,16]{1,0:T(8,128)(2,1)S(1)} all-reduce(f32[256,16]{1,0:T(8,128)S(1)} %get-tuple-element.1098), channel_id=1, replica_groups=mesh['head'=2,'outer'=4,'inner'=4] {'inner'}, use_global_device_ids=true, to_apply=%region_25.26 | all-reduce | flops 4096 | bytes 24576 | tf_op jit(solution)/shard_map/psum | solution.py:120
  162.9 0.8 convolution_bitcast_fusion.10
  163.9 12.2 %psum.55 = f32[16,128]{1,0:T(8,128)} all-reduce(f32[16,128]{1,0:T(8,128)S(1)} %fusion.91), channel_id=1, replica_groups=mesh['head'=2,'outer'=4,'inner'=4] {'outer'}, use_global_device_ids=true, to_apply=%region_26.27 | all-reduce | flops 2048 | bytes 16384 | tf_op jit(solution)/shard_map/psum | solution.py:206
  176.1 21.0 %all-reduce.5.cloned.1.call-done = f32[1024,16]{0,1:T(8,128)} async-done(((f32[1024,16]{0,1:T(8,128)}), f32[1024,16]{0,1:T(8,128)}) %all-reduce.5.cloned.1.call-update) | async-done | bytes 65552 | tf_op jit(solution)/shard_map/psum | solution.py:206
  (226 shorter events, 31.1 us)
Async XLA Ops:
  7.2 92.2 %copy-start = (bf16[256,1024]{1,0:T(8,128)(2,1)S(1)}, bf16[256,1024]{1,0:T(8,128)(2,1)}, u32[]{:S(2)}) copy-start(bf16[256,1024]{1,0:T(8,128)(2,1)} %param.25) | copy-start | bytes 1572868
  7.2 130.6 %all-reduce.7.cloned.1.call-start = ((), (), s32[]{:S(2)}) async-start(), calls=%async_computation.1 | async-start | bytes 262144 | tf_op jit(solution)/shard_map/psum | solution.py:190
  7.3 0.7 copy-start.2
  12.0 0.9 copy-start.3
  13.0 2.4 %copy-start.4 = (bf16[256,256]{1,0:T(8,128)(2,1)S(1)}, bf16[256,256]{1,0:T(8,128)(2,1)}, u32[]{:S(2)}) copy-start(bf16[256,256]{1,0:T(8,128)(2,1)} %param.24) | copy-start | bytes 393220
  13.2 0.7 copy-start.9
  15.7 10.6 %collective-permute-start = (bf16[128,128]{1,0:T(8,128)(2,1)S(1)}, bf16[128,128]{1,0:T(8,128)(2,1)S(1)}, u32[]{:S(2)}, u32[]{:S(2)}) collective-permute-start(bf16[128,128]{1,0:T(8,128)(2,1)S(1)} %copy.63), channel_id=1, source_target_pairs={{0,4},{4,8},{8,12},{12,0},{1,5},{5,9},{9,13},{13,1},{2,6},{6,10},{... | collective-permute-start | bytes 98312 | tf_op jit(solution)/shard_map/while/body/eval_jaxpr/ppermute | solution.py:13
  18.8 7.5 %collective-permute-start.1 = (bf16[128,128]{1,0:T(8,128)(2,1)S(1)}, bf16[128,128]{1,0:T(8,128)(2,1)S(1)}, u32[]{:S(2)}, u32[]{:S(2)}) collective-permute-start(bf16[128,128]{1,0:T(8,128)(2,1)S(1)} %copy.64), channel_id=1, source_target_pairs={{0,4},{4,8},{8,12},{12,0},{1,5},{5,9},{9,13},{13,1},{2,6},{6,10},{... | collective-permute-start | bytes 98312 | tf_op jit(solution)/shard_map/while/body/eval_jaxpr/ppermute | solution.py:13
  20.4 6.0 %collective-permute-start.2 = (bf16[128,128]{1,0:T(8,128)(2,1)S(1)}, bf16[128,128]{1,0:T(8,128)(2,1)S(1)}, u32[]{:S(2)}, u32[]{:S(2)}) collective-permute-start(bf16[128,128]{1,0:T(8,128)(2,1)S(1)} %copy.65), channel_id=1, source_target_pairs={{0,4},{4,8},{8,12},{12,0},{1,5},{5,9},{9,13},{13,1},{2,6},{6,10},{... | collective-permute-start | bytes 98312 | tf_op jit(solution)/shard_map/while/body/eval_jaxpr/ppermute | solution.py:13
  22.0 5.7 %collective-permute-start.3 = (bf16[128,128]{1,0:T(8,128)(2,1)S(1)}, bf16[128,128]{1,0:T(8,128)(2,1)S(1)}, u32[]{:S(2)}, u32[]{:S(2)}) collective-permute-start(bf16[128,128]{1,0:T(8,128)(2,1)S(1)} %copy.66), channel_id=1, source_target_pairs={{0,4},{4,8},{8,12},{12,0},{1,5},{5,9},{9,13},{13,1},{2,6},{6,10},{... | collective-permute-start | bytes 98312 | tf_op jit(solution)/shard_map/while/body/eval_jaxpr/ppermute | solution.py:13
  27.7 9.2 %collective-permute-start = (bf16[128,128]{1,0:T(8,128)(2,1)S(1)}, bf16[128,128]{1,0:T(8,128)(2,1)S(1)}, u32[]{:S(2)}, u32[]{:S(2)}) collective-permute-start(bf16[128,128]{1,0:T(8,128)(2,1)S(1)} %copy.63), channel_id=1, source_target_pairs={{0,4},{4,8},{8,12},{12,0},{1,5},{5,9},{9,13},{13,1},{2,6},{6,10},{... | collective-permute-start | bytes 98312 | tf_op jit(solution)/shard_map/while/body/eval_jaxpr/ppermute | solution.py:13
  28.2 8.8 %collective-permute-start.1 = (bf16[128,128]{1,0:T(8,128)(2,1)S(1)}, bf16[128,128]{1,0:T(8,128)(2,1)S(1)}, u32[]{:S(2)}, u32[]{:S(2)}) collective-permute-start(bf16[128,128]{1,0:T(8,128)(2,1)S(1)} %copy.64), channel_id=1, source_target_pairs={{0,4},{4,8},{8,12},{12,0},{1,5},{5,9},{9,13},{13,1},{2,6},{6,10},{... | collective-permute-start | bytes 98312 | tf_op jit(solution)/shard_map/while/body/eval_jaxpr/ppermute | solution.py:13
  29.8 7.2 %collective-permute-start.2 = (bf16[128,128]{1,0:T(8,128)(2,1)S(1)}, bf16[128,128]{1,0:T(8,128)(2,1)S(1)}, u32[]{:S(2)}, u32[]{:S(2)}) collective-permute-start(bf16[128,128]{1,0:T(8,128)(2,1)S(1)} %copy.65), channel_id=1, source_target_pairs={{0,4},{4,8},{8,12},{12,0},{1,5},{5,9},{9,13},{13,1},{2,6},{6,10},{... | collective-permute-start | bytes 98312 | tf_op jit(solution)/shard_map/while/body/eval_jaxpr/ppermute | solution.py:13
  31.4 5.7 %collective-permute-start.3 = (bf16[128,128]{1,0:T(8,128)(2,1)S(1)}, bf16[128,128]{1,0:T(8,128)(2,1)S(1)}, u32[]{:S(2)}, u32[]{:S(2)}) collective-permute-start(bf16[128,128]{1,0:T(8,128)(2,1)S(1)} %copy.66), channel_id=1, source_target_pairs={{0,4},{4,8},{8,12},{12,0},{1,5},{5,9},{9,13},{13,1},{2,6},{6,10},{... | collective-permute-start | bytes 98312 | tf_op jit(solution)/shard_map/while/body/eval_jaxpr/ppermute | solution.py:13
  37.1 9.2 %collective-permute-start = (bf16[128,128]{1,0:T(8,128)(2,1)S(1)}, bf16[128,128]{1,0:T(8,128)(2,1)S(1)}, u32[]{:S(2)}, u32[]{:S(2)}) collective-permute-start(bf16[128,128]{1,0:T(8,128)(2,1)S(1)} %copy.63), channel_id=1, source_target_pairs={{0,4},{4,8},{8,12},{12,0},{1,5},{5,9},{9,13},{13,1},{2,6},{6,10},{... | collective-permute-start | bytes 98312 | tf_op jit(solution)/shard_map/while/body/eval_jaxpr/ppermute | solution.py:13
  37.6 8.8 %collective-permute-start.1 = (bf16[128,128]{1,0:T(8,128)(2,1)S(1)}, bf16[128,128]{1,0:T(8,128)(2,1)S(1)}, u32[]{:S(2)}, u32[]{:S(2)}) collective-permute-start(bf16[128,128]{1,0:T(8,128)(2,1)S(1)} %copy.64), channel_id=1, source_target_pairs={{0,4},{4,8},{8,12},{12,0},{1,5},{5,9},{9,13},{13,1},{2,6},{6,10},{... | collective-permute-start | bytes 98312 | tf_op jit(solution)/shard_map/while/body/eval_jaxpr/ppermute | solution.py:13
  39.2 7.2 %collective-permute-start.2 = (bf16[128,128]{1,0:T(8,128)(2,1)S(1)}, bf16[128,128]{1,0:T(8,128)(2,1)S(1)}, u32[]{:S(2)}, u32[]{:S(2)}) collective-permute-start(bf16[128,128]{1,0:T(8,128)(2,1)S(1)} %copy.65), channel_id=1, source_target_pairs={{0,4},{4,8},{8,12},{12,0},{1,5},{5,9},{9,13},{13,1},{2,6},{6,10},{... | collective-permute-start | bytes 98312 | tf_op jit(solution)/shard_map/while/body/eval_jaxpr/ppermute | solution.py:13
  40.7 5.7 %collective-permute-start.3 = (bf16[128,128]{1,0:T(8,128)(2,1)S(1)}, bf16[128,128]{1,0:T(8,128)(2,1)S(1)}, u32[]{:S(2)}, u32[]{:S(2)}) collective-permute-start(bf16[128,128]{1,0:T(8,128)(2,1)S(1)} %copy.66), channel_id=1, source_target_pairs={{0,4},{4,8},{8,12},{12,0},{1,5},{5,9},{9,13},{13,1},{2,6},{6,10},{... | collective-permute-start | bytes 98312 | tf_op jit(solution)/shard_map/while/body/eval_jaxpr/ppermute | solution.py:13
  52.4 6.5 %collective-permute-start.8 = (bf16[256,1,128]{2,0,1:T(8,128)(2,1)S(1)}, bf16[256,1,128]{2,0,1:T(8,128)(2,1)S(1)}, u32[]{:S(2)}, u32[]{:S(2)}) collective-permute-start(bf16[256,1,128]{2,0,1:T(8,128)(2,1)S(1)} %convert_element_type.173), channel_id=1, source_target_pairs={{0,4},{4,8},{8,12},{12,0},{1,5},{5,9},{9,13},{13,1},{2,6},{6,10},{... | collective-permute-start | bytes 196616 | tf_op jit(solution)/shard_map/while/body/eval_jaxpr/ppermute | solution.py:13
  52.5 7.1 %collective-permute-start.9 = (bf16[256,1,128]{2,0,1:T(8,128)(2,1)S(1)}, bf16[256,1,128]{2,0,1:T(8,128)(2,1)S(1)}, u32[]{:S(2)}, u32[]{:S(2)}) collective-permute-start(bf16[256,1,128]{2,0,1:T(8,128)(2,1)S(1)} %convert_element_type.175), channel_id=1, source_target_pairs={{0,4},{4,8},{8,12},{12,0},{1,5},{5,9},{9,13},{13,1},{2,6},{6,10},{... | collective-permute-start | bytes 196616 | tf_op jit(solution)/shard_map/while/body/eval_jaxpr/ppermute | solution.py:13
  53.7 6.2 %collective-permute-start.4 = (bf16[128,128]{1,0:T(8,128)(2,1)S(1)}, bf16[128,128]{1,0:T(8,128)(2,1)S(1)}, u32[]{:S(2)}, u32[]{:S(2)}) collective-permute-start(bf16[128,128]{1,0:T(8,128)(2,1)S(1)} %copy.95), channel_id=1, source_target_pairs={{0,4},{4,8},{8,12},{12,0},{1,5},{5,9},{9,13},{13,1},{2,6},{6,10},{... | collective-permute-start | bytes 98312 | tf_op jit(solution)/shard_map/while/body/eval_jaxpr/ppermute | solution.py:13
  55.3 5.7 %collective-permute-start.5 = (bf16[128,128]{1,0:T(8,128)(2,1)S(1)}, bf16[128,128]{1,0:T(8,128)(2,1)S(1)}, u32[]{:S(2)}, u32[]{:S(2)}) collective-permute-start(bf16[128,128]{1,0:T(8,128)(2,1)S(1)} %copy.96), channel_id=1, source_target_pairs={{0,4},{4,8},{8,12},{12,0},{1,5},{5,9},{9,13},{13,1},{2,6},{6,10},{... | collective-permute-start | bytes 98312 | tf_op jit(solution)/shard_map/while/body/eval_jaxpr/ppermute | solution.py:13
  57.5 5.7 %collective-permute-start.6 = (bf16[128,128]{1,0:T(8,128)(2,1)S(1)}, bf16[128,128]{1,0:T(8,128)(2,1)S(1)}, u32[]{:S(2)}, u32[]{:S(2)}) collective-permute-start(bf16[128,128]{1,0:T(8,128)(2,1)S(1)} %copy.97), channel_id=1, source_target_pairs={{0,4},{4,8},{8,12},{12,0},{1,5},{5,9},{9,13},{13,1},{2,6},{6,10},{... | collective-permute-start | bytes 98312 | tf_op jit(solution)/shard_map/while/body/eval_jaxpr/ppermute | solution.py:13
  58.9 5.7 %collective-permute-start.7 = (bf16[128,128]{1,0:T(8,128)(2,1)S(1)}, bf16[128,128]{1,0:T(8,128)(2,1)S(1)}, u32[]{:S(2)}, u32[]{:S(2)}) collective-permute-start(bf16[128,128]{1,0:T(8,128)(2,1)S(1)} %copy.98), channel_id=1, source_target_pairs={{0,4},{4,8},{8,12},{12,0},{1,5},{5,9},{9,13},{13,1},{2,6},{6,10},{... | collective-permute-start | bytes 98312 | tf_op jit(solution)/shard_map/while/body/eval_jaxpr/ppermute | solution.py:13
  69.4 6.1 %collective-permute-start.8 = (bf16[256,1,128]{2,0,1:T(8,128)(2,1)S(1)}, bf16[256,1,128]{2,0,1:T(8,128)(2,1)S(1)}, u32[]{:S(2)}, u32[]{:S(2)}) collective-permute-start(bf16[256,1,128]{2,0,1:T(8,128)(2,1)S(1)} %convert_element_type.173), channel_id=1, source_target_pairs={{0,4},{4,8},{8,12},{12,0},{1,5},{5,9},{9,13},{13,1},{2,6},{6,10},{... | collective-permute-start | bytes 196616 | tf_op jit(solution)/shard_map/while/body/eval_jaxpr/ppermute | solution.py:13
  69.5 6.7 %collective-permute-start.9 = (bf16[256,1,128]{2,0,1:T(8,128)(2,1)S(1)}, bf16[256,1,128]{2,0,1:T(8,128)(2,1)S(1)}, u32[]{:S(2)}, u32[]{:S(2)}) collective-permute-start(bf16[256,1,128]{2,0,1:T(8,128)(2,1)S(1)} %convert_element_type.175), channel_id=1, source_target_pairs={{0,4},{4,8},{8,12},{12,0},{1,5},{5,9},{9,13},{13,1},{2,6},{6,10},{... | collective-permute-start | bytes 196616 | tf_op jit(solution)/shard_map/while/body/eval_jaxpr/ppermute | solution.py:13
  69.6 7.0 %collective-permute-start.4 = (bf16[128,128]{1,0:T(8,128)(2,1)S(1)}, bf16[128,128]{1,0:T(8,128)(2,1)S(1)}, u32[]{:S(2)}, u32[]{:S(2)}) collective-permute-start(bf16[128,128]{1,0:T(8,128)(2,1)S(1)} %copy.95), channel_id=1, source_target_pairs={{0,4},{4,8},{8,12},{12,0},{1,5},{5,9},{9,13},{13,1},{2,6},{6,10},{... | collective-permute-start | bytes 98312 | tf_op jit(solution)/shard_map/while/body/eval_jaxpr/ppermute | solution.py:13
  71.3 5.7 %collective-permute-start.5 = (bf16[128,128]{1,0:T(8,128)(2,1)S(1)}, bf16[128,128]{1,0:T(8,128)(2,1)S(1)}, u32[]{:S(2)}, u32[]{:S(2)}) collective-permute-start(bf16[128,128]{1,0:T(8,128)(2,1)S(1)} %copy.96), channel_id=1, source_target_pairs={{0,4},{4,8},{8,12},{12,0},{1,5},{5,9},{9,13},{13,1},{2,6},{6,10},{... | collective-permute-start | bytes 98312 | tf_op jit(solution)/shard_map/while/body/eval_jaxpr/ppermute | solution.py:13
  74.5 5.7 %collective-permute-start.6 = (bf16[128,128]{1,0:T(8,128)(2,1)S(1)}, bf16[128,128]{1,0:T(8,128)(2,1)S(1)}, u32[]{:S(2)}, u32[]{:S(2)}) collective-permute-start(bf16[128,128]{1,0:T(8,128)(2,1)S(1)} %copy.97), channel_id=1, source_target_pairs={{0,4},{4,8},{8,12},{12,0},{1,5},{5,9},{9,13},{13,1},{2,6},{6,10},{... | collective-permute-start | bytes 98312 | tf_op jit(solution)/shard_map/while/body/eval_jaxpr/ppermute | solution.py:13
  75.5 5.7 %collective-permute-start.7 = (bf16[128,128]{1,0:T(8,128)(2,1)S(1)}, bf16[128,128]{1,0:T(8,128)(2,1)S(1)}, u32[]{:S(2)}, u32[]{:S(2)}) collective-permute-start(bf16[128,128]{1,0:T(8,128)(2,1)S(1)} %copy.98), channel_id=1, source_target_pairs={{0,4},{4,8},{8,12},{12,0},{1,5},{5,9},{9,13},{13,1},{2,6},{6,10},{... | collective-permute-start | bytes 98312 | tf_op jit(solution)/shard_map/while/body/eval_jaxpr/ppermute | solution.py:13
  86.1 6.1 %collective-permute-start.8 = (bf16[256,1,128]{2,0,1:T(8,128)(2,1)S(1)}, bf16[256,1,128]{2,0,1:T(8,128)(2,1)S(1)}, u32[]{:S(2)}, u32[]{:S(2)}) collective-permute-start(bf16[256,1,128]{2,0,1:T(8,128)(2,1)S(1)} %convert_element_type.173), channel_id=1, source_target_pairs={{0,4},{4,8},{8,12},{12,0},{1,5},{5,9},{9,13},{13,1},{2,6},{6,10},{... | collective-permute-start | bytes 196616 | tf_op jit(solution)/shard_map/while/body/eval_jaxpr/ppermute | solution.py:13
  86.2 6.7 %collective-permute-start.9 = (bf16[256,1,128]{2,0,1:T(8,128)(2,1)S(1)}, bf16[256,1,128]{2,0,1:T(8,128)(2,1)S(1)}, u32[]{:S(2)}, u32[]{:S(2)}) collective-permute-start(bf16[256,1,128]{2,0,1:T(8,128)(2,1)S(1)} %convert_element_type.175), channel_id=1, source_target_pairs={{0,4},{4,8},{8,12},{12,0},{1,5},{5,9},{9,13},{13,1},{2,6},{6,10},{... | collective-permute-start | bytes 196616 | tf_op jit(solution)/shard_map/while/body/eval_jaxpr/ppermute | solution.py:13
  86.3 7.2 %collective-permute-start.4 = (bf16[128,128]{1,0:T(8,128)(2,1)S(1)}, bf16[128,128]{1,0:T(8,128)(2,1)S(1)}, u32[]{:S(2)}, u32[]{:S(2)}) collective-permute-start(bf16[128,128]{1,0:T(8,128)(2,1)S(1)} %copy.95), channel_id=1, source_target_pairs={{0,4},{4,8},{8,12},{12,0},{1,5},{5,9},{9,13},{13,1},{2,6},{6,10},{... | collective-permute-start | bytes 98312 | tf_op jit(solution)/shard_map/while/body/eval_jaxpr/ppermute | solution.py:13
  88.7 6.1 %collective-permute-start.5 = (bf16[128,128]{1,0:T(8,128)(2,1)S(1)}, bf16[128,128]{1,0:T(8,128)(2,1)S(1)}, u32[]{:S(2)}, u32[]{:S(2)}) collective-permute-start(bf16[128,128]{1,0:T(8,128)(2,1)S(1)} %copy.96), channel_id=1, source_target_pairs={{0,4},{4,8},{8,12},{12,0},{1,5},{5,9},{9,13},{13,1},{2,6},{6,10},{... | collective-permute-start | bytes 98312 | tf_op jit(solution)/shard_map/while/body/eval_jaxpr/ppermute | solution.py:13
  91.2 5.7 %collective-permute-start.6 = (bf16[128,128]{1,0:T(8,128)(2,1)S(1)}, bf16[128,128]{1,0:T(8,128)(2,1)S(1)}, u32[]{:S(2)}, u32[]{:S(2)}) collective-permute-start(bf16[128,128]{1,0:T(8,128)(2,1)S(1)} %copy.97), channel_id=1, source_target_pairs={{0,4},{4,8},{8,12},{12,0},{1,5},{5,9},{9,13},{13,1},{2,6},{6,10},{... | collective-permute-start | bytes 98312 | tf_op jit(solution)/shard_map/while/body/eval_jaxpr/ppermute | solution.py:13
  92.2 5.7 %collective-permute-start.7 = (bf16[128,128]{1,0:T(8,128)(2,1)S(1)}, bf16[128,128]{1,0:T(8,128)(2,1)S(1)}, u32[]{:S(2)}, u32[]{:S(2)}) collective-permute-start(bf16[128,128]{1,0:T(8,128)(2,1)S(1)} %copy.98), channel_id=1, source_target_pairs={{0,4},{4,8},{8,12},{12,0},{1,5},{5,9},{9,13},{13,1},{2,6},{6,10},{... | collective-permute-start | bytes 98312 | tf_op jit(solution)/shard_map/while/body/eval_jaxpr/ppermute | solution.py:13
  99.2 6.1 %collective-permute-start.11 = (bf16[256,1,128]{2,0,1:T(8,128)(2,1)S(1)}, bf16[256,1,128]{2,0,1:T(8,128)(2,1)S(1)}, u32[]{:S(2)}, u32[]{:S(2)}) collective-permute-start(bf16[256,1,128]{2,0,1:T(8,128)(2,1)S(1)} %convert_element_type.122), channel_id=1, source_target_pairs={{0,4},{4,8},{8,12},{12,0},{1,5},{5,9},{9,13},{13,1},{2,6},{6,10},{... | collective-permute-start | bytes 196616 | tf_op jit(solution)/shard_map/ppermute | solution.py:13
  99.3 0.8 copy-start.10
  99.3 6.7 %collective-permute-start.10 = (bf16[256,1,128]{2,0,1:T(8,128)(2,1)S(1)}, bf16[256,1,128]{2,0,1:T(8,128)(2,1)S(1)}, u32[]{:S(2)}, u32[]{:S(2)}) collective-permute-start(bf16[256,1,128]{2,0,1:T(8,128)(2,1)S(1)} %convert_element_type.119), channel_id=1, source_target_pairs={{0,4},{4,8},{8,12},{12,0},{1,5},{5,9},{9,13},{13,1},{2,6},{6,10},{... | collective-permute-start | bytes 196616 | tf_op jit(solution)/shard_map/ppermute | solution.py:13
  105.3 0.7 copy-start.6
  106.0 0.6 copy-start.7
  106.7 90.4 %all-reduce.5.cloned.1.call-start = ((), (), s32[]{:S(2)}) async-start(), calls=%async_computation | async-start | bytes 131072 | tf_op jit(solution)/shard_map/psum | solution.py:206
  137.8 0.9 copy-start.11
  138.6 25.1 %copy-start.1 = (bf16[256,128]{1,0:T(8,128)(2,1)}, bf16[256,128]{1,0:T(8,128)(2,1)S(1)}, u32[]{:S(2)}) copy-start(bf16[256,128]{1,0:T(8,128)(2,1)S(1)} %fusion.71) | copy-start | bytes 196612
  163.8 33.3 %copy-start.5 = (bf16[256,128]{1,0:T(8,128)(2,1)S(1)}, bf16[256,128]{1,0:T(8,128)(2,1)}, u32[]{:S(2)}) copy-start(bf16[256,128]{1,0:T(8,128)(2,1)} %get-tuple-element.1579) | copy-start | bytes 196612
  197.1 0.9 copy-start.8
Sparse Core Ops, SparseCore 0:
  106.8 30.8 all-reduce.6
  163.9 33.1 all-reduce.4
